TPU v7x, 16 devices: a 4x2x1 block of a 4x4x8 slice. The times are simulated.
16 devices in a mesh: data: 2 (over y, z), expert: 8 (over x, core).
Axes of the slice: x: 4, y: 2, z: 1, core: 2. Of those that a mesh axis runs over, the one named last changes fastest.
The devices are a block of a 4x4x8 slice.
Arguments:
- tok_x: bfloat16 [12288, 4096], P(('data', 'expert')), parts along dimension 0
- route_idx: int32 [12288, 2], P(('data', 'expert')), parts along dimension 0
- route_gate: float32 [12288, 2], P(('data', 'expert')), parts along dimension 0
- grad_y: bfloat16 [12288, 4096], P(('data', 'expert')), parts along dimension 0
- w_gate: bfloat16 [8, 4096, 1024], P('expert')
- w_up: bfloat16 [8, 4096, 1024], P('expert')
- w_down: bfloat16 [8, 1024, 4096], P('expert')
Outputs:
- output 1: bfloat16 [12288, 4096], P(('data', 'expert')), parts along dimension 0
- output 2: bfloat16 [12288, 4096], P(('data', 'expert')), parts along dimension 0
- output 3: float32 [16, 4096, 1024], P(('data', 'expert')), parts along dimension 0
- output 4: float32 [16, 4096, 1024], P(('data', 'expert')), parts along dimension 0
- output 5: float32 [16, 1024, 4096], P(('data', 'expert')), parts along dimension 0
There are 2 independent parts. A program takes and returns all parts, laid end to end along the dimension named above; an argument that names none is the same for every part.
All inputs are finite; a program needn't handle non-finite values.
Results may differ from a plain program's by a relative error of at most 0.00366429.
Values are sent between devices in bfloat16 or wider.
A program may use at most 768 MiB of HBM per device.

v0:
```python
import jax
import jax.numpy as jnp
from jax import lax
from jax.sharding import PartitionSpec as P


def silu_parts(pre_act):
    sigmoid_a = jax.nn.sigmoid(pre_act)
    return pre_act * sigmoid_a, sigmoid_a * (1.0 + pre_act * (1.0 - sigmoid_a))


def route_tables(local_idx, num_experts, capacity):
    tok_count, top_count = local_idx.shape
    slot_count = tok_count * top_count
    hot_stride = num_experts // min(4, num_experts // 8)
    flat_ids = local_idx.reshape(slot_count)
    onehot = (flat_ids[:, None] == jnp.arange(num_experts, dtype=jnp.int32)[None, :]).astype(jnp.int32)
    position = jnp.sum(jnp.cumsum(onehot, axis=0) * onehot, axis=1) - 1
    is_kept = (flat_ids % hot_stride != 0) & (position < capacity)
    dest_row = jnp.where(is_kept, flat_ids * capacity + position, num_experts * capacity)
    slot_src = jnp.full((num_experts * capacity + 1,), slot_count, jnp.int32).at[dest_row].set(jnp.arange(slot_count, dtype=jnp.int32))
    return dest_row, slot_src[:num_experts * capacity]


def expert_forward(rows_x, w_in, w_lin, w_out, form_set):
    x_form, w_form, h_form, out_form, dw_form = form_set
    wo_form = w_form[:-2] + 'fd'
    pre_a = jnp.einsum(x_form + ',' + w_form + '->' + h_form, rows_x, w_in, preferred_element_type=jnp.float32).astype(jnp.bfloat16)
    pre_b = jnp.einsum(x_form + ',' + w_form + '->' + h_form, rows_x, w_lin, preferred_element_type=jnp.float32).astype(jnp.bfloat16)
    hidden = (jax.nn.silu(pre_a.astype(jnp.float32)) * pre_b.astype(jnp.float32)).astype(jnp.bfloat16)
    out_rows = jnp.einsum(h_form + ',' + wo_form + '->' + out_form, hidden, w_out, preferred_element_type=jnp.float32).astype(jnp.bfloat16)
    return (pre_a, pre_b, hidden), out_rows


def expert_backward(rows_x, grad_out, saved, w_in, w_lin, w_out, form_set):
    x_form, w_form, h_form, out_form, dw_form = form_set
    wo_form = w_form[:-2] + 'fd'
    dwo_form = dw_form[:-2] + 'fd'
    pre_a, pre_b, hidden = saved
    silu_a, silu_slope = silu_parts(pre_a.astype(jnp.float32))
    lin_b = pre_b.astype(jnp.float32)
    grad_h = jnp.einsum(out_form + ',' + wo_form + '->' + h_form, grad_out, w_out, preferred_element_type=jnp.float32).astype(jnp.bfloat16).astype(jnp.float32)
    grad_a = (grad_h * lin_b * silu_slope).astype(jnp.bfloat16)
    grad_b = (grad_h * silu_a).astype(jnp.bfloat16)
    back_form = h_form + ',' + w_form + '->' + out_form
    grad_in = (jnp.einsum(back_form, grad_a, w_in, preferred_element_type=jnp.float32) + jnp.einsum(back_form, grad_b, w_lin, preferred_element_type=jnp.float32)).astype(jnp.bfloat16)
    dw_spec = x_form + ',' + h_form + '->' + dw_form
    grad_w_in = jnp.einsum(dw_spec, rows_x, grad_a, preferred_element_type=jnp.float32)
    grad_w_lin = jnp.einsum(dw_spec, rows_x, grad_b, preferred_element_type=jnp.float32)
    grad_w_out = jnp.einsum(h_form + ',' + out_form + '->' + dwo_form, hidden, grad_out, preferred_element_type=jnp.float32)
    return grad_in, grad_w_in, grad_w_lin, grad_w_out


def solution(mesh):
    group_n = mesh.shape['expert']
    tok_spec = P(('data', 'expert'))
    weight_spec = P('expert')

    def shard_body(tok_x, route_idx, route_gate, grad_y, w_gate, w_up, w_down):
        tok_count, model_dim = tok_x.shape
        top_count = route_idx.shape[1]
        local_count = w_gate.shape[0]
        num_experts = local_count * group_n
        hot_count = min(4, num_experts // 8)
        hot_stride = num_experts // hot_count
        capacity = max(4, 2 * tok_count * top_count // num_experts)
        flat_rows = num_experts * capacity
        my_rank = lax.axis_index('expert')
        owner_list = [(slot_n * hot_stride) // local_count for slot_n in range(hot_count)]
        local_list = [(slot_n * hot_stride) % local_count for slot_n in range(hot_count)]

        def hot_copy(weights):
            picked = [jnp.where(my_rank == owner_n, weights[local_n], jnp.zeros_like(weights[local_n])) for owner_n, local_n in zip(owner_list, local_list)]
            return lax.psum(jnp.stack(picked), 'expert')

        hot_wg = hot_copy(w_gate)
        hot_wu = hot_copy(w_up)
        hot_wd = hot_copy(w_down)
        dest_row, slot_src = route_tables(route_idx, num_experts, capacity)
        tok_src = slot_src // top_count
        zero_row = jnp.zeros((1, model_dim), jnp.bfloat16)
        buf_shape = (group_n, local_count, capacity, model_dim)
        send_x = jnp.concatenate([tok_x, zero_row])[tok_src].reshape(buf_shape)
        recv_x = lax.all_to_all(send_x, 'expert', 0, 0)
        cold_forms = ('gecd', 'edf', 'gecf', 'gecd', 'edf')
        hot_forms = ('td', 'hdf', 'htf', 'htd', 'hdf')
        cold_saved, cold_out = expert_forward(recv_x, w_gate, w_up, w_down, cold_forms)
        back_out = lax.all_to_all(cold_out, 'expert', 0, 0)
        hot_saved, hot_out = expert_forward(tok_x, hot_wg, hot_wu, hot_wd, hot_forms)
        hot_ids = jnp.arange(hot_count, dtype=jnp.int32) * hot_stride
        hot_gate = jnp.sum(jnp.where(route_idx[None, :, :] == hot_ids[:, None, None], route_gate[None, :, :], 0.0), axis=2)
        out_slots = jnp.concatenate([back_out.reshape(flat_rows, model_dim), zero_row])[dest_row].reshape(tok_count, top_count, model_dim)
        out_y = jnp.sum(route_gate[:, :, None] * out_slots.astype(jnp.float32), axis=1) + jnp.sum(hot_gate[:, :, None] * hot_out.astype(jnp.float32), axis=0)
        gate_pad = jnp.concatenate([route_gate.reshape(tok_count * top_count), jnp.zeros((1,), jnp.float32)])
        send_gate = gate_pad[slot_src].reshape(group_n, local_count, capacity)
        send_dy = jnp.concatenate([grad_y, zero_row])[tok_src].reshape(buf_shape)
        recv_gate = lax.all_to_all(send_gate, 'expert', 0, 0)
        recv_dy = lax.all_to_all(send_dy, 'expert', 0, 0)
        cold_grad_out = (recv_gate[..., None] * recv_dy.astype(jnp.float32)).astype(jnp.bfloat16)
        cold_dx, cold_dwg, cold_dwu, cold_dwd = expert_backward(recv_x, cold_grad_out, cold_saved, w_gate, w_up, w_down, cold_forms)
        back_dx = lax.all_to_all(cold_dx, 'expert', 0, 0)
        hot_grad_out = (hot_gate[:, :, None] * grad_y.astype(jnp.float32)[None]).astype(jnp.bfloat16)
        hot_dx, hot_dwg, hot_dwu, hot_dwd = expert_backward(tok_x, hot_grad_out, hot_saved, hot_wg, hot_wu, hot_wd, hot_forms)
        dx_slots = jnp.concatenate([back_dx.reshape(flat_rows, model_dim), zero_row])[dest_row].reshape(tok_count, top_count, model_dim)
        grad_x = jnp.sum(dx_slots.astype(jnp.float32), axis=1) + jnp.sum(hot_dx.astype(jnp.float32), axis=0)
        hot_sums = lax.psum((hot_dwg, hot_dwu, hot_dwd), 'expert')
        grad_list = []
        for cold_w, hot_w in zip((cold_dwg, cold_dwu, cold_dwd), hot_sums):
            for slot_n in range(hot_count):
                cold_w = cold_w.at[local_list[slot_n]].add(jnp.where(my_rank == owner_list[slot_n], hot_w[slot_n], 0.0))
            grad_list.append(cold_w)
        return out_y.astype(jnp.bfloat16), grad_x.astype(jnp.bfloat16), grad_list[0], grad_list[1], grad_list[2]

    return jax.shard_map(shard_body, mesh=mesh, in_specs=(tok_spec, tok_spec, tok_spec, tok_spec, weight_spec, weight_spec, weight_spec), out_specs=(tok_spec, tok_spec, tok_spec, tok_spec, tok_spec), check_vma=False)
```

profile of v0, /device:TPU:112, one launch (start us, length us, event | category | flops | bytes accessed | tf_op | source)
XLA Modules:
  0.0 2346.7 jit_solution(5049743246982638972)
XLA Ops:
  19.9 30.6 %gather_fusion.2 = f32[3072]{0:T(1024)} fusion(f32[1537]{0:T(1024)S(1)} %pad_maximum_fusion, s32[3072]{0:T(1024)S(1)} %get-tuple-element.47), kind=kCustom, calls=%fused_computation.2 | custom fusion | bytes 36864 | tf_op jit(solution)/shard_map/gather | solution.py:95
  62.0 45.9 %gather_fusion = bf16[3072,4096]{1,0:T(8,128)(2,1)} fusion(bf16[769,4096]{1,0:T(8,128)(2,1)} %concatenate.21, s32[3072]{0:T(1024)S(1)} %get-tuple-element.48), kind=kCustom, calls=%fused_computation | custom fusion | bytes 50343936 | tf_op jit(solution)/shard_map/gather | solution.py:83
  140.5 45.9 %gather_fusion.3 = bf16[3072,4096]{1,0:T(8,128)(2,1)} fusion(bf16[769,4096]{1,0:T(8,128)(2,1)} %concatenate.24, s32[3072]{0:T(1024)S(1)} %get-tuple-element.48), kind=kCustom, calls=%fused_computation.3 | custom fusion | bytes 50343936 | tf_op jit(solution)/shard_map/gather | solution.py:96
  186.5 448.2 %all-reduce.11.cloned.1.call-done = (bf16[1024,4096]{1,0:T(8,128)(2,1)}, bf16[4096,1024]{1,0:T(8,128)(2,1)}, bf16[4096,1024]{1,0:T(8,128)(2,1)}) async-done(((bf16[1024,4096]{1,0:T(8,128)(2,1)}, bf16[4096,1024]{1,0:T(8,128)(2,1)}, bf16[4096,1024]{1,0:T(8,128)(2,1)}), (bf16[1024,4096]{1,0:T(8,128)(2,1)}, bf16[4096,1024]{1,0:T(8,128)(2,1)}, bf16[4096,1024]{1,0:T(8,128)(2,1)})) %all-reduce.11.cloned.1.call-update) | async-done | bytes 25165840 | tf_op jit(solution)/shard_map/psum | solution.py:74
  707.2 33.0 %fusion.48 = bf16[8,384,1024]{2,1,0:T(8,128)(2,1)} fusion(bf16[1,4096,1024]{2,1,0:T(8,128)(2,1)} %param.17, bf16[8,1,384,4096]{3,2,1,0:T(8,128)(2,1)} %all-to-all-done), kind=kOutput, calls=%fused_computation.68 | convolution fusion | flops 25772949504 | bytes 39845888 | tf_op jit(solution)/shard_map/gecd,edf->gecf/dot_general | solution.py:28
  740.2 33.2 %fusion.53 = bf16[8,384,1024]{2,1,0:T(8,128)(2,1)} fusion(bf16[1,4096,1024]{2,1,0:T(8,128)(2,1)} %param.18, bf16[8,1,384,4096]{3,2,1,0:T(8,128)(2,1)} %all-to-all-done), kind=kOutput, calls=%fused_computation.69 | convolution fusion | flops 25772949504 | bytes 39845888 | tf_op jit(solution)/shard_map/gecd,edf->gecf/dot_general | solution.py:29
  773.4 35.4 %convert_bitcast_fusion = bf16[8,1,384,4096]{3,2,1,0:T(8,128)(2,1)} fusion(bf16[1,1024,4096]{2,1,0:T(8,128)(2,1)} %param.19, bf16[8,384,1024]{2,1,0:T(8,128)(2,1)} %fusion.53, bf16[8,384,1024]{2,1,0:T(8,128)(2,1)} %fusion.48), kind=kOutput, calls=%fused_computation.19 | convolution fusion | flops 25807552512 | bytes 46137344 | tf_op jit(solution)/shard_map/gecf,efd->gecd/dot_general | solution.py:31
  808.8 224.3 %all-to-all-done.3 = bf16[8,1,384,4096]{3,2,1,0:T(8,128)(2,1)} async-done(((bf16[8,1,384,4096]{3,2,1,0:T(8,128)(2,1)}), bf16[8,1,384,4096]{3,2,1,0:T(8,128)(2,1)}, u32[]{:S(2)}, u32[]{:S(2)}) %all-to-all-start.3) | async-done | bytes 25165856 | tf_op jit(solution)/shard_map/all_to_all | solution.py:98
  1055.3 33.3 %fusion.43 = bf16[8,384,1024]{2,1,0:T(8,128)(2,1)} fusion(bf16[1,1024,4096]{2,1,0:T(8,128)(2,1)} %param.19, bf16[8,1,384,4096]{3,2,1,0:T(8,128)(2,1)} %all-to-all-done.3, f32[8,384]{1,0:T(8,128)S(1)} %bitcast.336), kind=kOutput, calls=%fused_computation.67 | convolution fusion | flops 25810698240 | bytes 39858176 | tf_op jit(solution)/shard_map/gecd,efd->gecf/dot_general | solution.py:42
  1088.6 39.6 %fusion.36 = f32[8,384,4096]{2,1,0:T(8,128)} fusion(bf16[1,4096,1024]{2,1,0:T(8,128)(2,1)} %param.17, bf16[8,384,1024]{2,1,0:T(8,128)(2,1)} %fusion.43, bf16[8,384,1024]{2,1,0:T(8,128)(2,1)} %fusion.53, bf16[8,384,1024]{2,1,0:T(8,128)(2,1)} %fusion.48), kind=kOutput, calls=%fused_computation.54 | convolution fusion | flops 25810698240 | bytes 77594624 | tf_op jit(solution)/shard_map/gecf,edf->gecd/dot_general | solution.py:46
  1128.1 39.1 %fusion.1 = bf16[8,1,384,4096]{3,2,1,0:T(8,128)(2,1)} fusion(f32[8,384,4096]{2,1,0:T(8,128)} %fusion.36, bf16[1,4096,1024]{2,1,0:T(8,128)(2,1)} %param.18, bf16[8,384,1024]{2,1,0:T(8,128)(2,1)} %fusion.43, bf16[8,384,1024]{2,1,0:T(8,128)(2,1)} %fusion.48), kind=kOutput, calls=%fused_computation.9 | convolution fusion | flops 25820135424 | bytes 96468992 | tf_op jit(solution)/shard_map/gecf,edf->gecd/dot_general | solution.py:46
  1167.2 267.0 %all-to-all-done.1 = bf16[8,1,384,4096]{3,2,1,0:T(8,128)(2,1)} async-done(((bf16[8,1,384,4096]{3,2,1,0:T(8,128)(2,1)}), bf16[8,1,384,4096]{3,2,1,0:T(8,128)(2,1)}, u32[]{:S(2)}, u32[]{:S(2)}) %all-to-all-start.1) | async-done | bytes 25165856 | tf_op jit(solution)/shard_map/all_to_all | solution.py:88
  1441.0 497.8 %all-reduce.9.cloned.1.call-done = (f32[1,4096,1024]{2,1,0:T(8,128)}, f32[1,4096,1024]{2,1,0:T(8,128)}, f32[1,1024,4096]{2,1,0:T(8,128)}) async-done(((f32[1,4096,1024]{2,1,0:T(8,128)}, f32[1,4096,1024]{2,1,0:T(8,128)}, f32[1,1024,4096]{2,1,0:T(8,128)}), (f32[1,4096,1024]{2,1,0:T(8,128)}, f32[1,4096,1024]{2,1,0:T(8,128)}, f32[1,1024,4096]{2,1,0:T(8,128)})) %all-reduce.9.cloned.1.call-update) | async-done | bytes 50331664 | tf_op jit(solution)/shard_map/psum | solution.py:106
  1938.7 37.8 %fusion.15 = f32[1,4096,1024]{2,1,0:T(8,128)} fusion(f32[1,4096,1024]{2,1,0:T(8,128)} %get-tuple-element.42, bf16[8,1,384,4096]{3,2,1,0:T(8,128)(2,1)} %all-to-all-done, pred[]{:T(512)S(6)} %eq.52, bf16[8,384,1024]{2,1,0:T(8,128)(2,1)} %fusion.43, bf16[8,384,1024]{2,1,0:T(8,128)(2,1)} %fusion.48), kind=kOutput, calls=%fused_computation.28 | convolution fusion | flops 25803358208 | bytes 71303168 | tf_op jit(solution)/shard_map/gecd,gecf->edf/dot_general | solution.py:49
  1976.5 43.1 %fusion.16 = f32[1,4096,1024]{2,1,0:T(8,128)} fusion(f32[1,4096,1024]{2,1,0:T(8,128)} %get-tuple-element.41, bf16[8,1,384,4096]{3,2,1,0:T(8,128)(2,1)} %all-to-all-done, pred[]{:T(512)S(6)} %eq.52, bf16[8,384,1024]{2,1,0:T(8,128)(2,1)} %fusion.43, bf16[8,384,1024]{2,1,0:T(8,128)(2,1)} %fusion.53, bf16[8,384,1024]{2,1,0:T(8,128)(2,1)} %fusion.48), kind=kOutput, calls=%fused_computation.30 | convolution fusion | flops 25819086848 | bytes 77594624 | tf_op jit(solution)/shard_map/gecd,gecf->edf/dot_general | solution.py:48
  2019.6 46.6 %fusion.14 = f32[1,1024,4096]{2,1,0:T(8,128)} fusion(f32[1,1024,4096]{2,1,0:T(8,128)} %get-tuple-element.43, bf16[8,1,384,4096]{3,2,1,0:T(8,128)(2,1)} %all-to-all-done.3, f32[8,384]{1,0:T(8,128)S(1)} %bitcast.337, pred[]{:T(512)S(6)} %eq.52, bf16[8,384,1024]{2,1,0:T(8,128)(2,1)} %fusion.53, bf16[8,384,1024]{2,1,0:T(8,128)(2,1)} %fusion.48), kind=kOutput, calls=%fused_computation.26 | convolution fusion | flops 25841106944 | bytes 71315456 | tf_op jit(solution)/shard_map/gecf,gecd->efd/dot_general | solution.py:50
  2066.2 21.0 concatenate.22
  2087.2 33.8 %gather_fusion.1 = bf16[1536,4096]{1,0:T(8,128)(2,1)} fusion(bf16[3073,4096]{1,0:T(8,128)(2,1)} %concatenate.22, s32[2048]{0:T(1024)S(1)} %copy-done.2), kind=kCustom, calls=%fused_computation.1 | custom fusion | bytes 25171968 | tf_op jit(solution)/shard_map/gather | solution.py:92
  2120.9 26.7 %reshape.397 = f32[768,2,4096]{2,1,0:T(2,128)} reshape(bf16[1536,4096]{1,0:T(8,128)(2,1)} %gather_fusion.1) | data formatting | bytes 37748736 | tf_op jit(solution)/shard_map/convert_element_type | solution.py:93
  2147.6 41.2 %multiply_reduce_fusion = f32[768,4096]{1,0:T(8,128)} fusion(f32[768,2,4096]{2,1,0:T(2,128)} %reshape.397, f32[768,2]{1,0:T(8,128)S(1)} %copy-done.1), kind=kLoop, calls=%fused_computation.18 | loop fusion | flops 9437184 | bytes 37754880 | tf_op jit(solution)/shard_map/reduce_sum | solution.py:93
  2203.4 21.2 concatenate.25
  2224.6 33.6 %gather_fusion.4 = bf16[1536,4096]{1,0:T(8,128)(2,1)} fusion(bf16[3073,4096]{1,0:T(8,128)(2,1)} %concatenate.25, s32[2048]{0:T(1024)S(1)} %copy-done.2), kind=kCustom, calls=%fused_computation.4 | custom fusion | bytes 25171968 | tf_op jit(solution)/shard_map/gather | solution.py:104
  2258.1 26.6 %reshape.398 = f32[768,2,4096]{2,1,0:T(2,128)} reshape(bf16[1536,4096]{1,0:T(8,128)(2,1)} %gather_fusion.4) | data formatting | bytes 37748736 | tf_op jit(solution)/shard_map/convert_element_type | solution.py:105
  2284.8 36.9 %reduce_sum.41 = f32[768,4096]{1,0:T(8,128)} reduce(f32[768,2,4096]{2,1,0:T(2,128)} %reshape.398, f32[]{:T(128)} %constant.125.clone.1), dimensions={1}, to_apply=%region_9.10 | reduce | flops 3145728 | bytes 37748740 | tf_op jit(solution)/shard_map/reduce_sum | solution.py:105
  (98 shorter events, 190.3 us)
Async XLA Ops:
  50.4 57.5 %all-to-all-start.2 = ((f32[8,1,384]{2,1,0:T(1,128)}), f32[8,1,384]{2,1,0:T(1,128)S(1)}, u32[]{:S(2)}, u32[]{:S(2)}) async-start(f32[8,1,384]{2,1,0:T(1,128)} %bitcast.33), calls=%async_computation.2 | async-start | bytes 24576 | tf_op jit(solution)/shard_map/all_to_all | solution.py:97
  108.5 538.1 %all-to-all-start = ((bf16[8,1,384,4096]{3,2,1,0:T(8,128)(2,1)}), bf16[8,1,384,4096]{3,2,1,0:T(8,128)(2,1)}, u32[]{:S(2)}, u32[]{:S(2)}) async-start(bf16[8,1,384,4096]{3,2,1,0:T(8,128)(2,1)} %bitcast.329), calls=%async_computation | async-start | bytes 50331648 | tf_op jit(solution)/shard_map/all_to_all | solution.py:84
  115.1 519.6 %all-reduce.11.cloned.1.call-start = ((), (), s32[]{:S(2)}) async-start(), calls=%async_computation.6 | async-start | bytes 50331648 | tf_op jit(solution)/shard_map/psum | solution.py:74
  140.5 45.9 %copy-start.7 = (s32[768,2]{0,1:T(2,128)S(1)}, s32[768,2]{0,1:T(2,128)}, u32[]{:S(2)}) copy-start(s32[768,2]{0,1:T(2,128)} %param.14) | copy-start | bytes 18436
  140.5 45.9 %copy-start.8 = (f32[768,2]{0,1:T(2,128)S(1)}, f32[768,2]{0,1:T(2,128)}, u32[]{:S(2)}) copy-start(f32[768,2]{0,1:T(2,128)} %param.15) | copy-start | bytes 18436
  186.5 509.8 %copy-start.11 = (f32[768]{0:T(1024)}, f32[768]{0:T(1024)S(1)}, u32[]{:S(2)}) copy-start(f32[768]{0:T(1024)S(1)} %fusion.96) | copy-start | bytes 9220
  646.6 386.5 %all-to-all-start.3 = ((bf16[8,1,384,4096]{3,2,1,0:T(8,128)(2,1)}), bf16[8,1,384,4096]{3,2,1,0:T(8,128)(2,1)}, u32[]{:S(2)}, u32[]{:S(2)}) async-start(bf16[8,1,384,4096]{3,2,1,0:T(8,128)(2,1)} %bitcast.330), calls=%async_computation.3 | async-start | bytes 50331648 | tf_op jit(solution)/shard_map/all_to_all | solution.py:98
  653.4 1285.4 %all-reduce.9.cloned.1.call-start = ((), (), s32[]{:S(2)}) async-start(), calls=%async_computation.5 | async-start | bytes 100663296 | tf_op jit(solution)/shard_map/psum | solution.py:106
  665.2 20.0 copy-start.19
  665.2 31.1 %slice-start.2 = ((s8[6291456]{0:T(1024)(128)(4,1)}), s8[4194304]{0:T(1024)(128)(4,1)S(1)}, s32[]{:S(2)}) async-start(s8[6291456]{0:T(1024)(128)(4,1)} %bitcast.333), calls=%async_computation.9 | async-start | bytes 8388608
  675.8 20.5 slice-start.3
  808.8 231.3 %copy-start.6 = (s32[1536]{0:T(1024)S(1)}, s32[1536]{0:T(1024)}, u32[]{:S(2)}) copy-start(s32[1536]{0:T(1024)} %copy-done.5) | copy-start | bytes 18436
  808.8 232.0 %copy-start.4 = (f32[8,1,384]{2,1,0:T(1,128)S(1)}, f32[8,1,384]{2,1,0:T(1,128)}, u32[]{:S(2)}) copy-start(f32[8,1,384]{2,1,0:T(1,128)} %copy-done.3) | copy-start | bytes 36868
  808.8 232.0 %copy-start.14 = (bf16[1024,768]{1,0:T(8,128)(2,1)S(1)}, bf16[1024,768]{1,0:T(8,128)(2,1)}, u32[]{:S(2)}) copy-start(bf16[1024,768]{1,0:T(8,128)(2,1)} %convolution_convert_fusion.2) | copy-start | bytes 4718596
  808.8 232.0 %copy-start.17 = (bf16[1024,768]{1,0:T(8,128)(2,1)S(1)}, bf16[1024,768]{1,0:T(8,128)(2,1)}, u32[]{:S(2)}) copy-start(bf16[1024,768]{1,0:T(8,128)(2,1)} %copy-done.16) | copy-start | bytes 4718596
  1033.1 401.0 %all-to-all-start.1 = ((bf16[8,1,384,4096]{3,2,1,0:T(8,128)(2,1)}), bf16[8,1,384,4096]{3,2,1,0:T(8,128)(2,1)}, u32[]{:S(2)}, u32[]{:S(2)}) async-start(bf16[8,1,384,4096]{3,2,1,0:T(8,128)(2,1)} %convert_bitcast_fusion), calls=%async_computation.1 | async-start | bytes 50331648 | tf_op jit(solution)/shard_map/all_to_all | solution.py:88
  1434.2 769.2 %all-to-all-start.4 = ((bf16[8,1,384,4096]{3,2,1,0:T(8,128)(2,1)}), bf16[8,1,384,4096]{3,2,1,0:T(8,128)(2,1)}, u32[]{:S(2)}, u32[]{:S(2)}) async-start(bf16[8,1,384,4096]{3,2,1,0:T(8,128)(2,1)} %fusion.1), calls=%async_computation.4 | async-start | bytes 50331648 | tf_op jit(solution)/shard_map/all_to_all | solution.py:101
  1976.5 43.1 %copy-start.10 = (f32[8,1,384]{2,0,1:T(8,128)S(1)}, f32[8,1,384]{2,0,1:T(8,128)}, u32[]{:S(2)}) copy-start(f32[8,1,384]{2,0,1:T(8,128)} %copy-done.9) | copy-start | bytes 36868
  2066.2 21.0 copy-start.2
  2120.9 26.7 %copy-start.1 = (f32[768,2]{1,0:T(8,128)S(1)}, f32[768,2]{1,0:T(8,128)}, u32[]{:S(2)}) copy-start(f32[768,2]{1,0:T(8,128)} %copy-done) | copy-start | bytes 18436
  2147.6 41.2 %copy-start.12 = (f32[768]{0:T(1024)S(1)}, f32[768]{0:T(1024)}, u32[]{:S(2)}) copy-start(f32[768]{0:T(1024)} %copy-done.11) | copy-start | bytes 9220
  2147.6 41.2 %copy-start.15 = (bf16[1024,768]{1,0:T(8,128)(2,1)S(1)}, bf16[1024,768]{1,0:T(8,128)(2,1)}, u32[]{:S(2)}) copy-start(bf16[1024,768]{1,0:T(8,128)(2,1)} %convolution_convert_fusion.2) | copy-start | bytes 4718596
  2147.6 41.2 %copy-start.18 = (bf16[1024,768]{1,0:T(8,128)(2,1)S(1)}, bf16[1024,768]{1,0:T(8,128)(2,1)}, u32[]{:S(2)}) copy-start(bf16[1024,768]{1,0:T(8,128)(2,1)} %copy-done.16) | copy-start | bytes 4718596
  2284.8 36.9 %copy-start.20 = (bf16[768,1024]{0,1:T(8,128)(2,1)S(1)}, bf16[768,1024]{0,1:T(8,128)(2,1)}, u32[]{:S(2)}) copy-start(bf16[768,1024]{0,1:T(8,128)(2,1)} %copy-done.19) | copy-start | bytes 4718596
  (8 other events, 74.4 us)
Sparse Core Ops, SparseCore 0:
  134.3 500.3 all-reduce.10
  707.3 1231.3 all-reduce.8
where the time goes:
time: 2350 us
  waiting for transfers between devices  1440 us (61%)
  matrix products  453 us (19%)
  local copies, waits for them, and re-layouts  308 us (13%)
  other arithmetic  100 us (4%)
  starting transfers between devices  33.2 us (1%)
    psum x1, waiting for transfers between devices, shard_body(): hot_sums = lax.psum((hot_dwg, hot_dwu, hot_dwd), 'expert')  498 us
    psum x1, waiting for transfers between devices, hot_copy(): return lax.psum(jnp.stack(picked), 'expert')  448 us
    all_to_all x1, waiting for transfers between devices, shard_body(): back_out = lax.all_to_all(cold_out, 'expert', 0, 0)  267 us
    all_to_all x1, waiting for transfers between devices, shard_body(): recv_dy = lax.all_to_all(send_dy, 'expert', 0, 0)  224 us
    dot_general x2, matrix products, expert_backward(): jnp.einsum(h_form + ',' + out_form + '->' + dwo_form, hidden, grad_out, p...  57.4 us
    dot_general x2, matrix products, expert_backward(): jnp.einsum(back_form, grad_b, w_lin, preferred_element_type=jnp.float32)  56.7 us
    dot_general x2, matrix products, expert_backward(): jnp.einsum(dw_spec, rows_x, grad_a, preferred_element_type=jnp.float32)  54.2 us
    dot_general x2, matrix products, expert_backward(): jnp.einsum(back_form, grad_a, w_in, preferred_element_type=jnp.float32)  54.1 us
  transfers between devices with their start and end apart: 7, of which 4 were waited for; matrix products, arithmetic and copies ran while one was open for 29% of the time, Pallas kernels for 0%

commit v1 on v0

v1 whole, which is shorter than its diff:
```python
import jax
import jax.numpy as jnp
from jax import lax
from jax.sharding import PartitionSpec as P

BF = jnp.bfloat16
F32 = jnp.float32


def dot(form, a, b):
    return jnp.einsum(form, a, b, preferred_element_type=F32)


def expert_rows(x, dy, gate, w1, w3, w2):
    pre_a = dot('cd,df->cf', x, w1).astype(BF)
    pre_b = dot('cd,df->cf', x, w3).astype(BF)
    a = pre_a.astype(F32)
    b = pre_b.astype(F32)
    sig = jax.nn.sigmoid(a)
    silu = a * sig
    slope = sig * (1.0 + a * (1.0 - sig))
    hid = (silu * b).astype(BF)
    out = dot('cf,fd->cd', hid, w2).astype(BF)
    live = (gate > 0.0)[:, None]
    g = (gate[:, None] * dy.astype(F32)).astype(BF)
    dh = dot('cd,fd->cf', g, w2).astype(BF).astype(F32)
    da = jnp.where(live, dh * b * slope, 0.0).astype(BF)
    db = jnp.where(live, dh * silu, 0.0).astype(BF)
    hid = jnp.where(live, hid, jnp.zeros_like(hid))
    dx = (dot('cf,df->cd', da, w1) + dot('cf,df->cd', db, w3)).astype(BF)
    dw1 = dot('cd,cf->df', x, da)
    dw3 = dot('cd,cf->df', x, db)
    dw2 = dot('cf,cd->fd', hid, g)
    return out, dx, dw1, dw3, dw2


def solution(mesh):
    group = mesh.shape['expert']
    tok_spec = P(('data', 'expert'))
    w_spec = P('expert')

    def body(tok_x, route_idx, route_gate, grad_y, w_gate, w_up, w_down):
        toks, dim = tok_x.shape
        tops = route_idx.shape[1]
        slots = toks * tops
        local = w_gate.shape[0]
        experts = local * group
        stride = experts // min(4, experts // 8)
        cap = max(4, 2 * slots // experts)
        w1, w3, w2 = w_gate[0], w_up[0], w_down[0]

        flat = route_idx.reshape(slots)
        onehot = (flat[:, None] == jnp.arange(experts, dtype=jnp.int32)[None, :]).astype(jnp.int32)
        pos = jnp.sum(jnp.cumsum(onehot, axis=0) * onehot, axis=1) - 1
        is_hot = flat % stride == 0
        slot_ids = jnp.arange(slots, dtype=jnp.int32)
        flat_gate = route_gate.reshape(slots)

        def tables(first):
            kept = (pos >= first) & (pos < first + cap)
            if first:
                kept = kept & is_hot
            dest = jnp.where(kept, flat * cap + pos - first, experts * cap)
            src = jnp.full((experts * cap + 1,), slots, jnp.int32).at[dest].set(slot_ids)[:experts * cap]
            live = src < slots
            src = jnp.where(live, src, 0)
            gate = jnp.where(live, flat_gate[src], 0.0)
            row = (src // tops).astype(F32)
            table = jnp.stack([row.reshape(experts, cap), gate.reshape(experts, cap)], axis=1)
            table = lax.all_to_all(table, 'expert', 0, 0)
            base = jnp.arange(group, dtype=jnp.int32)[:, None] * toks
            rows = (table[:, 0].astype(jnp.int32) + base).reshape(group * cap)
            return kept, jnp.where(kept, dest, 0), rows, table[:, 1].reshape(group * cap)

        def slot_sum(back, kept, dest, weight):
            rows = back.reshape(group * cap, dim)[dest].astype(F32)
            if weight is not None:
                rows = rows * weight[:, None]
            rows = jnp.where(kept[:, None], rows, 0.0).reshape(toks, tops, dim)
            return jnp.sum(rows, axis=1)

        all_x = lax.all_gather(tok_x, 'expert', tiled=True)
        all_dy = lax.all_gather(grad_y, 'expert', tiled=True)

        def run_pass(first):
            kept, dest, rows, gate = tables(first)
            out, dx, dw1, dw3, dw2 = expert_rows(all_x[rows], all_dy[rows], gate, w1, w3, w2)
            back_out = lax.all_to_all(out.reshape(group, cap, dim), 'expert', 0, 0)
            back_dx = lax.all_to_all(dx.reshape(group, cap, dim), 'expert', 0, 0)
            y = slot_sum(back_out, kept, dest, flat_gate)
            gx = slot_sum(back_dx, kept, dest, None)
            return y, gx, dw1, dw3, dw2

        first = run_pass(0)
        hot_most = jnp.max(jnp.where(is_hot, pos, 0))
        spill = lax.pmax(hot_most, ('data', 'expert')) >= cap
        y, gx, dw1, dw3, dw2 = first
        res = lax.cond(
            spill,
            lambda f: tuple(u + v for u, v in zip(f, run_pass(cap))),
            lambda f: f, first)
        y, gx, dw1, dw3, dw2 = res
        return y.astype(BF), gx.astype(BF), dw1[None], dw3[None], dw2[None]

    return jax.shard_map(body, mesh=mesh, in_specs=(tok_spec,) * 4 + (w_spec,) * 3, out_specs=(tok_spec,) * 5, check_vma=False)
```

time: 2350 us -> 1590 us (0.68)
  waiting for transfers between devices: 1440 us -> 191 us
  blocking collectives: 0 us -> 305 us
  local copies, waits for them, and re-layouts: 308 us -> 476 us
  matrix products: 453 us -> 347 us
  starting transfers between devices: 33.2 us -> 122 us
    psum x2 -> x0, waiting for transfers between devices: 946 us -> none  [the longest x1 498 us: shard_body(): hot_sums = lax.psum((hot_dwg, hot_dwu, hot_dwd), 'expert')]
    all_to_all x5 -> x3, waiting for transfers between devices: 491 us -> 5.23 us  [the longest x1 5.22 us: tables(): table = lax.all_to_all(table, 'expert', 0, 0)]
    pmax x0 -> x1, blocking collectives: none -> 305 us  [body(): spill = lax.pmax(hot_most, ('data', 'expert')) >= cap]
    gather x5, local copies, waits for them, and re-layouts: 190 us -> 413 us  [the longest x1 167 us: run_pass(): all_x[rows]]
    all_gather x0 -> x2, waiting for transfers between devices: none -> 185 us  [the longest x1 185 us: body(): all_x = lax.all_gather(tok_x, 'expert', tiled=True)]
    dot_general x18 -> x9, matrix products: 453 us -> 347 us  [dot(): return jnp.einsum(form, a, b, preferred_element_type=F32)]
    all_to_all x5 -> x3, starting transfers between devices: 32.4 us -> 121 us  [the longest x1 59.3 us: run_pass(): back_out = lax.all_to_all(out.reshape(group, cap, dim), 'expert', 0, 0)]
    concatenate x4 -> x0, local copies, waits for them, and re-layouts: 54.8 us -> none  [the longest x1 21.2 us: shard_body(): jnp.concatenate([back_dx.reshape(flat_rows, model_dim), zero_row])[dest_row]]
  transfers between devices with their start and end apart: 7 -> 5, of which waited for: 4 -> 2; matrix products, arithmetic and copies ran while one was open for 29% -> 49% of each run, Pallas kernels for 0% -> 0%
where the time goes in v1:
time: 1590 us; the launch traced here: 1570 us
  local copies, waits for them, and re-layouts  476 us (30%)
  matrix products  347 us (22%)
  blocking collectives  305 us (19%)
  waiting for transfers between devices  191 us (12%)
  starting transfers between devices  122 us (8%)
  other arithmetic  112 us (7%)
    dot_general x9, matrix products, dot(): return jnp.einsum(form, a, b, preferred_element_type=F32)  347 us
    pmax x1, blocking collectives, body(): spill = lax.pmax(hot_most, ('data', 'expert')) >= cap  305 us
    all_gather x1, waiting for transfers between devices, body(): all_x = lax.all_gather(tok_x, 'expert', tiled=True)  185 us
    gather x1, local copies, waits for them, and re-layouts, run_pass(): all_x[rows]  167 us
    gather x1, local copies, waits for them, and re-layouts, run_pass(): all_dy[rows]  162 us
    reduce_sum x1, other arithmetic, slot_sum(): return jnp.sum(rows, axis=1)  88 us
    gather x2, local copies, waits for them, and re-layouts, slot_sum(): rows = back.reshape(group * cap, dim)[dest].astype(F32)  67.2 us
    all_to_all x1, starting transfers between devices, run_pass(): back_out = lax.all_to_all(out.reshape(group, cap, dim), 'expert', 0, 0)  59.3 us
  transfers between devices with their start and end apart: 5, of which 2 were waited for; matrix products, arithmetic and copies ran while one was open for 49% of the time, Pallas kernels for 0%

profile of v1, /device:TPU:112, one launch (start us, length us, event | category | flops | bytes accessed | tf_op | source)
XLA Modules:
  0.0 1570.3 jit_solution(4913879920478137565)
XLA Ops:
  15.8 6.2 scatter_custom_fusion.1
  22.0 17.4 %gather_fusion.5 = f32[3072]{0:T(1024)S(1)} fusion(f32[1536]{0:T(1024)S(1)} %reshape.427, s32[3072]{0:T(1024)S(1)} %get-tuple-element.182), kind=kCustom, calls=%fused_computation.5 | custom fusion | bytes 36864 | tf_op jit(solution)/shard_map/gather | solution.py:67
  51.9 184.8 %all-gather.3.cloned.1.call-done = bf16[6144,4096]{1,0:T(8,128)(2,1)} async-done(((bf16[768,4096]{1,0:T(8,128)(2,1)}), bf16[6144,4096]{1,0:T(8,128)(2,1)}) %all-gather.3.cloned.1.call-update) | async-done | bytes 50331664 | tf_op jit(solution)/shard_map/all_gather | solution.py:82
  236.7 166.8 %gather_fusion.6 = bf16[3072,4096]{1,0:T(8,128)(2,1)} fusion(bf16[6144,4096]{1,0:T(8,128)(2,1)} %all-gather.3.cloned.1.call-done, s32[3072]{0:T(1024)S(1)} %broadcast_clamp_fusion.1), kind=kCustom, calls=%fused_computation.6 | custom fusion | bytes 50343936 | tf_op jit(solution)/shard_map/gather | solution.py:87
  403.5 33.0 %convolution_convert_fusion.5 = bf16[3072,1024]{1,0:T(8,128)(2,1)} fusion(bf16[3072,4096]{1,0:T(8,128)(2,1)} %gather_fusion.6, bf16[1,4096,1024]{2,1,0:T(8,128)(2,1)} %param.13), kind=kOutput, calls=%fused_computation.101 | convolution fusion | flops 25772949504 | bytes 39845888 | tf_op jit(solution)/shard_map/cd,df->cf/dot_general | solution.py:11
  436.5 33.0 %convolution_convert_fusion.4 = bf16[3072,1024]{1,0:T(8,128)(2,1)} fusion(bf16[3072,4096]{1,0:T(8,128)(2,1)} %gather_fusion.6, bf16[1,4096,1024]{2,1,0:T(8,128)(2,1)} %param.14), kind=kOutput, calls=%fused_computation.100 | convolution fusion | flops 25772949504 | bytes 39845888 | tf_op jit(solution)/shard_map/cd,df->cf/dot_general | solution.py:11
  469.5 35.9 %convolution_convert_fusion.3 = bf16[3072,4096]{1,0:T(8,128)(2,1)} fusion(bf16[1,1024,4096]{2,1,0:T(8,128)(2,1)} %param.15, bf16[3072,1024]{1,0:T(8,128)(2,1)} %convolution_convert_fusion.4, bf16[3072,1024]{1,0:T(8,128)(2,1)} %convolution_convert_fusion.5), kind=kOutput, calls=%fused_computation.77 | convolution fusion | flops 25807552512 | bytes 46137344 | tf_op jit(solution)/shard_map/cf,fd->cd/dot_general | solution.py:11
  505.3 59.3 %all-to-all-start.4 = ((bf16[8,384,4096]{2,1,0:T(8,128)(2,1)}), bf16[8,384,4096]{2,1,0:T(8,128)(2,1)}, u32[]{:S(2)}, u32[]{:S(2)}) async-start(bf16[8,384,4096]{2,1,0:T(8,128)(2,1)} %bitcast.90), calls=%async_computation.4 | async-start | bytes 50331648 | tf_op jit(solution)/shard_map/all_to_all | solution.py:88
  564.7 161.6 %gather_fusion.8 = bf16[3072,4096]{1,0:T(8,128)(2,1)} fusion(bf16[6144,4096]{1,0:T(8,128)(2,1)} %all-gather.5.cloned.1.call-done, s32[3072]{0:T(1024)S(1)} %copy-done.16), kind=kCustom, calls=%fused_computation.8 | custom fusion | bytes 50343936 | tf_op jit(solution)/shard_map/gather | solution.py:87
  726.3 33.6 %fusion.46 = bf16[3072,1024]{1,0:T(8,128)(2,1)} fusion(bf16[3072,4096]{1,0:T(8,128)(2,1)} %gather_fusion.8, f32[3072]{0:T(1024)S(1)} %bitcast.101, bf16[1,1024,4096]{2,1,0:T(8,128)(2,1)} %param.15), kind=kOutput, calls=%fused_computation.99 | convolution fusion | flops 25810698240 | bytes 39858176 | tf_op jit(solution)/shard_map/cd,fd->cf/dot_general | solution.py:11
  759.8 40.4 %fusion.64 = f32[3072,4096]{1,0:T(8,128)} fusion(bf16[1,4096,1024]{2,1,0:T(8,128)(2,1)} %param.13, bf16[3072,1024]{1,0:T(8,128)(2,1)} %convolution_convert_fusion.4, bf16[3072,1024]{1,0:T(8,128)(2,1)} %fusion.46, bf16[3072,1024]{1,0:T(8,128)(2,1)} %convolution_convert_fusion.5, pred[3072]{0:T(1024)(128)(4,1)S(1)} %broadcast_compare_fusion.1), kind=kOutput, calls=%fused_computation.154 | convolution fusion | flops 25813843968 | bytes 77597696 | tf_op jit(solution)/shard_map/cf,df->cd/dot_general | solution.py:11
  800.2 40.1 %add_convert_fusion.1 = bf16[3072,4096]{1,0:T(8,128)(2,1)} fusion(f32[3072,4096]{1,0:T(8,128)} %fusion.64, bf16[1,4096,1024]{2,1,0:T(8,128)(2,1)} %param.14, bf16[3072,1024]{1,0:T(8,128)(2,1)} %fusion.46, pred[3072]{0:T(1024)(128)(4,1)S(1)} %broadcast_compare_fusion.1, bf16[3072,1024]{1,0:T(8,128)(2,1)} %convolution_convert_fusion.5), kind=kOutput, calls=%fused_computation.73 | convolution fusion | flops 25823281152 | bytes 96472064 | tf_op jit(solution)/shard_map/cf,df->cd/dot_general | solution.py:11
  840.3 56.4 %all-to-all-start.5 = ((bf16[8,384,4096]{2,1,0:T(8,128)(2,1)}), bf16[8,384,4096]{2,1,0:T(8,128)(2,1)}, u32[]{:S(2)}, u32[]{:S(2)}) async-start(bf16[8,384,4096]{2,1,0:T(8,128)(2,1)} %bitcast.88), calls=%async_computation.5 | async-start | bytes 50331648 | tf_op jit(solution)/shard_map/all_to_all | solution.py:89
  896.7 305.2 %pmax.7 = s32[]{:T(128)} all-reduce(s32[]{:T(128)} %get-tuple-element.178), channel_id=1, replica_groups=mesh['data'=2,'expert'=8] {'data','expert'}, use_global_device_ids=true, to_apply=%region_4.5 | all-reduce | flops 1 | bytes 8 | tf_op jit(solution)/shard_map/pmax | solution.py:96
  1204.4 40.8 %fusion.70 = f32[4096,1024]{1,0:T(8,128)} fusion(bf16[3072,4096]{1,0:T(8,128)(2,1)} %gather_fusion.6, bf16[3072,1024]{1,0:T(8,128)(2,1)} %fusion.46, pred[3072]{0:T(1024)(128)(4,1)S(1)} %broadcast_compare_fusion.1, bf16[3072,1024]{1,0:T(8,128)(2,1)} %convolution_convert_fusion.5), kind=kOutput, calls=%fused_computation.158 | convolution fusion | flops 25798115328 | bytes 54529024 | tf_op jit(solution)/shard_map/cd,cf->df/dot_general | solution.py:11
  1245.3 47.9 %fusion.73 = f32[4096,1024]{1,0:T(8,128)} fusion(bf16[3072,4096]{1,0:T(8,128)(2,1)} %gather_fusion.6, bf16[3072,1024]{1,0:T(8,128)(2,1)} %convolution_convert_fusion.4, bf16[3072,1024]{1,0:T(8,128)(2,1)} %fusion.46, bf16[3072,1024]{1,0:T(8,128)(2,1)} %convolution_convert_fusion.5, pred[3072]{0:T(1024)(128)(4,1)S(1)} %broadcast_compare_fusion.1), kind=kOutput, calls=%fused_computation.159 | convolution fusion | flops 25813843968 | bytes 60820480 | tf_op jit(solution)/shard_map/cd,cf->df/dot_general | solution.py:11
  1293.1 42.6 %fusion.42 = f32[1024,4096]{1,0:T(8,128)} fusion(bf16[3072,4096]{1,0:T(8,128)(2,1)} %gather_fusion.8, f32[3072]{0:T(1024)S(1)} %bitcast.102, pred[3072]{0:T(1024)(128)(4,1)S(1)} %broadcast_compare_fusion.1, bf16[3072,1024]{1,0:T(8,128)(2,1)} %convolution_convert_fusion.4, bf16[3072,1024]{1,0:T(8,128)(2,1)} %convolution_convert_fusion.5), kind=kOutput, calls=%fused_computation.95 | convolution fusion | flops 25835864064 | bytes 54541312 | tf_op jit(solution)/shard_map/cf,cd->fd/dot_general | solution.py:11
  1335.7 33.7 %gather_fusion.7 = bf16[1536,4096]{1,0:T(8,128)(2,1)} fusion(bf16[3072,4096]{1,0:T(8,128)(2,1)} %bitcast.24, s32[2048]{0:T(1024)S(1)} %copy-done.19), kind=kCustom, calls=%fused_computation.7 | custom fusion | bytes 25171968 | tf_op jit(solution)/shard_map/gather | solution.py:76
  1369.4 26.6 %reshape.434 = f32[768,2,4096]{2,1,0:T(2,128)} reshape(bf16[1536,4096]{1,0:T(8,128)(2,1)} %gather_fusion.7) | data formatting | bytes 37748736 | tf_op jit(solution)/shard_map/convert_element_type | solution.py:76
  1396.0 33.5 %gather_fusion.9 = bf16[1536,4096]{1,0:T(8,128)(2,1)} fusion(bf16[3072,4096]{1,0:T(8,128)(2,1)} %bitcast.27, s32[2048]{0:T(1024)S(1)} %copy-done.19), kind=kCustom, calls=%fused_computation.9 | custom fusion | bytes 25171968 | tf_op jit(solution)/shard_map/gather | solution.py:76
  1429.5 26.9 %reshape.435 = f32[768,2,4096]{2,1,0:T(2,128)} reshape(bf16[1536,4096]{1,0:T(8,128)(2,1)} %gather_fusion.9) | data formatting | bytes 37748736 | tf_op jit(solution)/shard_map/convert_element_type | solution.py:76
  1456.5 88.0 %select_reduce_fusion.2 = (f32[768,4096]{1,0:T(8,128)}, f32[768,4096]{1,0:T(8,128)}) fusion(f32[768,2,4096]{2,1,0:T(2,128)} %reshape.435, pred[768,2]{1,0:T(8,128)(4,1)S(1)} %copy-done.9, f32[768,2,4096]{2,1,0:T(2,128)} %reshape.434, f32[768,2]{1,0:T(8,128)S(1)} %copy-done.4), kind=kLoop, calls=%fused_computation.75 | loop fusion | flops 25165824 | bytes 75505152 | tf_op jit(solution)/shard_map/reduce_sum | solution.py:80
  1546.8 8.2 convert_element_type.206
  1555.1 8.2 convert_element_type.207
  (87 shorter events, 25.2 us)
Async XLA Ops:
  7.2 1.6 copy-start.26
  7.2 7.5 copy-start.27
  7.2 229.5 %all-gather.3.cloned.1.call-start = ((), (), s32[]{:S(2)}) async-start(), calls=%async_computation.6 | async-start | bytes 56623104 | tf_op jit(solution)/shard_map/all_gather | solution.py:82
  8.0 556.7 %all-gather.5.cloned.1.call-start = ((), (), s32[]{:S(2)}) async-start(), calls=%async_computation.7 | async-start | bytes 56623104 | tf_op jit(solution)/shard_map/all_gather | solution.py:83
  9.2 3.4 copy-start.10
  14.9 388.6 %copy-start.3 = (f32[768,2]{1,0:T(8,128)}, f32[768,2]{1,0:T(8,128)S(1)}, u32[]{:S(2)}) copy-start(f32[768,2]{1,0:T(8,128)S(1)} %copy.23) | copy-start | bytes 18436
  15.1 388.4 %copy-start = (f32[1536]{0:T(1024)}, f32[1536]{0:T(1024)S(1)}, u32[]{:S(2)}) copy-start(f32[1536]{0:T(1024)S(1)} %reshape.427) | copy-start | bytes 18436
  40.2 11.1 all-to-all-start.3
  51.9 351.6 %copy-start.15 = (s32[3072]{0:T(1024)}, s32[3072]{0:T(1024)S(1)}, u32[]{:S(2)}) copy-start(s32[3072]{0:T(1024)S(1)} %broadcast_clamp_fusion.1) | copy-start | bytes 36868
  505.3 59.3 %copy-start.20 = (f32[8,1,384]{2,1,0:T(1,128)S(1)}, f32[8,1,384]{2,1,0:T(1,128)}, u32[]{:S(2)}) copy-start(f32[8,1,384]{2,1,0:T(1,128)} %get-tuple-element.179) | copy-start | bytes 36868
  505.3 59.4 %copy-start.16 = (s32[3072]{0:T(1024)S(1)}, s32[3072]{0:T(1024)}, u32[]{:S(2)}) copy-start(s32[3072]{0:T(1024)} %copy-done.15) | copy-start | bytes 36868
  505.3 334.9 %all-to-all-start.4 = ((bf16[8,384,4096]{2,1,0:T(8,128)(2,1)}), bf16[8,384,4096]{2,1,0:T(8,128)(2,1)}, u32[]{:S(2)}, u32[]{:S(2)}) async-start(bf16[8,384,4096]{2,1,0:T(8,128)(2,1)} %bitcast.90), calls=%async_computation.4 | async-start | bytes 50331648 | tf_op jit(solution)/shard_map/all_to_all | solution.py:88
  840.3 362.2 %copy-start.24 = (s32[1536]{0:T(1024)S(1)}, s32[1536]{0:T(1024)}, u32[]{:S(2)}) copy-start(s32[1536]{0:T(1024)} %get-tuple-element.169) | copy-start | bytes 18436
  840.3 362.8 %copy-start.11 = (s32[1536]{0:T(1024)S(1)}, s32[1536]{0:T(1024)}, u32[]{:S(2)}) copy-start(s32[1536]{0:T(1024)} %copy-done.10) | copy-start | bytes 18436
  840.3 363.4 %copy-start.6 = (s32[768,2]{1,0:T(8,128)S(1)}, s32[768,2]{1,0:T(8,128)}, u32[]{:S(2)}) copy-start(s32[768,2]{1,0:T(8,128)} %copy-done.5) | copy-start | bytes 18436
  840.3 555.7 %all-to-all-start.5 = ((bf16[8,384,4096]{2,1,0:T(8,128)(2,1)}), bf16[8,384,4096]{2,1,0:T(8,128)(2,1)}, u32[]{:S(2)}, u32[]{:S(2)}) async-start(bf16[8,384,4096]{2,1,0:T(8,128)(2,1)} %bitcast.88), calls=%async_computation.5 | async-start | bytes 50331648 | tf_op jit(solution)/shard_map/all_to_all | solution.py:89
  1245.3 47.9 %copy-start.21 = (f32[8,1,384]{2,1,0:T(1,128)S(1)}, f32[8,1,384]{2,1,0:T(1,128)}, u32[]{:S(2)}) copy-start(f32[8,1,384]{2,1,0:T(1,128)} %get-tuple-element.179) | copy-start | bytes 36868
  1293.1 42.6 %copy-start.19 = (s32[2048]{0:T(1024)S(1)}, s32[2048]{0:T(1024)}, u32[]{:S(2)}) copy-start(s32[2048]{0:T(1024)} %pad_clamp_fusion.1) | copy-start | bytes 24580
  1429.5 26.9 %copy-start.4 = (f32[768,2]{1,0:T(8,128)S(1)}, f32[768,2]{1,0:T(8,128)}, u32[]{:S(2)}) copy-start(f32[768,2]{1,0:T(8,128)} %copy-done.3) | copy-start | bytes 18436
  1429.5 26.9 %copy-start.9 = (pred[768,2]{1,0:T(8,128)(4,1)S(1)}, pred[768,2]{1,0:T(8,128)(4,1)}, u32[]{:S(2)}) copy-start(pred[768,2]{1,0:T(8,128)(4,1)} %compare_and_fusion) | copy-start | bytes 4612
  1456.4 88.1 %copy-start.1 = (f32[1536]{0:T(1024)S(1)}, f32[1536]{0:T(1024)}, u32[]{:S(2)}) copy-start(f32[1536]{0:T(1024)} %copy-done) | copy-start | bytes 18436
  1456.4 88.1 %copy-start.12 = (s32[1536]{0:T(1024)S(1)}, s32[1536]{0:T(1024)}, u32[]{:S(2)}) copy-start(s32[1536]{0:T(1024)} %copy-done.10) | copy-start | bytes 18436
  1456.4 88.1 %copy-start.14 = (s32[1536]{0:T(1024)S(1)}, s32[1536]{0:T(1024)}, u32[]{:S(2)}) copy-start(s32[1536]{0:T(1024)} %copy-done.13) | copy-start | bytes 18436
  1456.5 88.1 %copy-start.23 = (s32[1536]{0:T(1024)S(1)}, s32[1536]{0:T(1024)}, u32[]{:S(2)}) copy-start(s32[1536]{0:T(1024)} %negate_select_fusion.2) | copy-start | bytes 18436
  (2 other events, 1.5 us)
Sparse Core Ops, SparseCore 0:
  9.6 227.0 all-gather.2
  238.3 223.5 all-gather.4
